TPU v7x, 16 devices: a whole 2x2x2 slice. The times are simulated.
16 devices in a mesh: dp: 1, sp: 16 (over x, y, z, core).
Axes of the slice: x: 2, y: 2, z: 2, core: 2. Of those that a mesh axis runs over, the one named last changes fastest.
Arguments:
- q: bfloat16 [32, 32, 64], P('dp')
- k: bfloat16 [32, 8192, 32, 64], P('dp', 'sp')
- v: bfloat16 [32, 8192, 32, 64], P('dp', 'sp')
Outputs:
- q: bfloat16 [32, 32, 64], P('dp')
All inputs are finite; a program needn't handle non-finite values.
Results may differ from a plain program's by a relative error of at most 0.012.
Values are sent between devices in bfloat16 or wider.
A program may use at most 2 GiB of HBM per device.

v0:
```python
import jax
import jax.numpy as jnp
from jax import lax
from jax.sharding import PartitionSpec as P


def einsum(form, a, b):
    return jnp.einsum(form, a.astype(jnp.float32), b.astype(jnp.float32))


def part_of(q, k, v):
    grouped = q.reshape(q.shape[0], k.shape[2], -1, q.shape[2])
    scores = einsum("bgsd,bugd->bgsu", grouped, k) * q.shape[2] ** -0.5
    high = jnp.max(scores, -1, keepdims=True)
    weights = jnp.exp(scores - high)
    seen = einsum("bgsu,bugd->bgsd", weights.astype(jnp.bfloat16), v)
    return jnp.concatenate([seen, jnp.sum(weights, -1, keepdims=True), high], -1)


def together(parts):
    seen, total, high = parts[..., :-2], parts[..., -2:-1], parts[..., -1:]
    scale = jnp.exp(high - jnp.max(high, 0))
    return (jnp.sum(seen * scale, 0) / jnp.sum(total * scale, 0)).astype(jnp.bfloat16)


def solution(mesh):
    def step(q, k, v):
        return together(lax.all_gather(part_of(q, k, v), "sp")).reshape(q.shape)

    return jax.shard_map(
        step,
        mesh=mesh,
        in_specs=(P("dp", None, None), P("dp", "sp", None, None), P("dp", "sp", None, None)),
        out_specs=P("dp", None, None),
        check_vma=False,
    )
```

profile of v0, /device:TPU:0, one launch (start us, length us, event | category | flops | bytes accessed | tf_op | source)
XLA Modules:
  0.0 141.3 jit_solution(5198168167253406307)
XLA Ops:
  6.5 0.0 all-gather.3.cloned.1.call-start
  6.5 22.7 %fusion.7 = f32[32,32,1,512]{3,2,1,0:T(1,128)S(1)} fusion(bf16[32,512,32,64]{1,3,2,0:T(8,128)(2,1)} %param.4, bf16[32,32,64,1]{2,1,0,3:T(8,128)(2,1)} %bitcast.26), kind=kOutput, calls=%fused_computation.12 | convolution fusion | flops 67108864 | bytes 69337088 | tf_op jit(solution)/shard_map/bgsd,bugd->bgsu/dot_general | solution.py:8
  29.3 0.2 fusion.5
  29.5 0.6 fusion.6
  30.1 0.3 copy.17
  30.4 0.3 copy.16
  30.6 25.6 %fusion.1 = f32[32,32,1,64]{3,2,1,0:T(1,128)S(1)} fusion(bf16[32,512,32,64]{1,3,2,0:T(8,128)(2,1)} %param.5, bf16[32,32,512,1]{2,1,0,3:T(8,128)(2,1)S(1)} %get-tuple-element.7), kind=kOutput, calls=%fused_computation.3 | convolution fusion | flops 67108864 | bytes 68419584 | tf_op jit(solution)/shard_map/bgsu,bugd->bgsd/dot_general | solution.py:8
  56.2 1.2 pad_maximum_fusion
  57.4 0.0 all-gather.3.cloned.1.call-update
  57.4 51.6 %all-gather.3.cloned.1.call-done = f32[512,32,1,66]{3,1,2,0:T(8,128)} async-done(((f32[32,32,1,66]{3,1,2,0:T(8,128)}), f32[512,32,1,66]{3,1,2,0:T(8,128)}) %all-gather.3.cloned.1.call-update) | async-done | bytes 4325392 | tf_op jit(solution)/shard_map/all_gather | solution.py:28
  109.0 13.7 %copy.18 = f32[512,32,1,66]{1,0,3,2:T(8,128)} copy(f32[512,32,1,66]{3,1,2,0:T(8,128)} %all-gather.3.cloned.1.call-done) | data formatting | bytes 8650752 | tf_op jit(solution)/shard_map/all_gather | solution.py:28
  122.8 1.0 slice_reduce_fusion
  123.7 1.1 fusion.9
  124.8 8.2 %fusion = f32[32,32,64]{1,0,2:T(8,128)S(1)} fusion(f32[16,32,32,1,66]{2,1,0,4,3:T(8,128)} %bitcast.25, f32[16,32,32]{2,1,0:T(8,128)S(1)} %get-tuple-element.6), kind=kLoop, calls=%fused_computation.1 | loop fusion | flops 2031616 | bytes 4521984 | tf_op jit(solution)/shard_map/reduce_sum | solution.py:23
  133.0 0.1 divide_convert_fusion
  133.2 1.3 copy.19
Async XLA Ops:
  6.5 102.5 %all-gather.3.cloned.1.call-start = ((), (), s32[]{:S(2)}) async-start(), calls=%async_computation | async-start | bytes 8912896 | tf_op jit(solution)/shard_map/all_gather | solution.py:28
Sparse Core Ops, SparseCore 0:
  57.5 51.4 all-gather.2
where the time goes:
time: 142 us; the launch traced here: 141 us
  waiting for transfers between devices  51.6 us (36%)
  matrix products  48.3 us (34%)
  local copies, waits for them, and re-layouts  15.5 us (11%)
  between operations  13.4 us (9%)
  other arithmetic  12.4 us (9%)
    all_gather x1, waiting for transfers between devices, step(): return together(lax.all_gather(part_of(q, k, v), 'sp')).reshape(q.shape)  51.6 us
    dot_general x2, matrix products, einsum(): return jnp.einsum(form, a.astype(jnp.float32), b.astype(jnp.float32))  48.3 us
    all_gather x1, local copies, waits for them, and re-layouts, step(): return together(lax.all_gather(part_of(q, k, v), 'sp')).reshape(q.shape)  13.7 us
    reduce_sum x1, other arithmetic, together(): jnp.sum(seen * scale, 0) / jnp.sum(total * scale, 0)  8.2 us
  transfers between devices with their start and end apart: 1, of which 1 were waited for; matrix products, arithmetic and copies ran while one was open for 0% of the time, Pallas kernels for 0%

commit v1 on v0

v1 whole, which is shorter than its diff:
```python
import jax
import jax.numpy as jnp
from jax import lax
from jax.experimental import pallas as pl
from jax.experimental.pallas import tpu as pltpu
from jax.sharding import PartitionSpec as P

MESH = pl.DeviceIdType.MESH
BF16, F32 = jnp.bfloat16, jnp.float32

DEV = 16
SEQ = 32
HEADS = 32
HEAD = 64
RUN = 512
HALF = 16
ROWS = HALF * HEAD
GROUP = 4
GROUPS = SEQ // GROUP
LAG = 8
AHEAD = LAG // GROUP
SLOTS = 8


def peers(me):
    bits = [(me // 2**i) % 2 for i in range(4)]
    for flip in (14, 15, 12, 10, 6, 13, 11, 7, 8, 4, 2, 9, 5, 3, 1):
        yield sum((1 - bit if flip >> i & 1 else bit) * 2**i for i, bit in enumerate(bits))


def kernel(q_ref, k_ref, v_ref, out_ref, kbuf, vbuf, ebuf, stats, parts, ksem, vsem, stat_send, stat_recv, part_send, part_recv):
    me = lax.axis_index("sp")
    row = lax.broadcasted_iota(jnp.int32, (HALF, 128), 0)
    lane = lax.broadcasted_iota(jnp.int32, (HALF, 128), 1)

    def k_copy(b, slot):
        return pltpu.make_async_copy(k_ref.at[b], kbuf.at[slot], ksem.at[slot])

    def v_copy(b, slot):
        return pltpu.make_async_copy(v_ref.at[b], vbuf.at[slot], vsem.at[slot])

    def send(ref, send_sem, recv_sem):
        for peer in peers(me):
            pltpu.make_async_remote_copy(ref, ref, send_sem, recv_sem, device_id={"sp": peer}, device_id_type=MESH).start()

    def wait_peers(ref, sem):
        some = ref.at[pl.ds(0, DEV - 1)]
        pltpu.make_async_copy(some, some, sem).wait()

    def scores(b, slot, i, rows):
        highs, sums = rows
        k_copy(b, slot).wait()
        for g in range(2):
            query = q_ref[b, HALF * g : HALF * (g + 1), :].astype(F32)
            query = jnp.concatenate([query, query], -1)
            query = jnp.where(lane // HEAD == row % 2, query, 0.0)
            query = jnp.concatenate([jnp.where(row // 2 == c, query, 0.0).astype(BF16) for c in range(HALF // 2)], -1)
            score = jnp.dot(query, kbuf[slot, ROWS * g : ROWS * (g + 1), :], preferred_element_type=F32) * HEAD**-0.5
            high = jnp.max(score, -1, keepdims=True)
            weight = jnp.exp(score - high)
            ebuf[b, g] = weight
            here = lane // HALF == 2 * i + g
            highs = jnp.where(here, high, highs)
            sums = jnp.where(here, jnp.sum(weight, -1, keepdims=True), sums)
        return highs, sums

    def exchange(g, rows):
        mine = lane % HALF == row
        for i, x in enumerate(rows):
            stats[g, me, :, 128 * i : 128 * (i + 1)] = jnp.sum(jnp.where(mine, x, 0.0), 0, keepdims=True)
        send(stats.at[g, me], stat_send.at[g], stat_recv.at[g])

    def shares(g):
        wait_peers(stats.at[g], stat_recv.at[g])
        high = stats[g, :, :, 0:128]
        top = jnp.max(high, 0)
        total = jnp.sum(stats[g, :, :, 128:256] * jnp.exp(high - top[None]), 0)
        return jnp.exp(stats[g, me, :, 0:128] - top) / total

    def values(b, slot, i, share):
        v_copy(b, slot).wait()
        halves = []
        for g in range(2):
            scale = jnp.sum(jnp.where(lane == HALF * (2 * i + g) + row, share, 0.0), -1, keepdims=True)
            weight = (ebuf[b, g] * scale).astype(BF16)
            seen = jnp.zeros((HALF, 128), F32)
            for c in range(0, HALF // 2, 2):
                first = ROWS * g + 128 * c
                wide = lax.dot_general(weight, vbuf[slot, first : first + 256, :], (((1,), (1,)), ((), ())), preferred_element_type=F32)
                seen = jnp.where(row // 2 == c, wide[:, :128], seen)
                seen = jnp.where(row // 2 == c + 1, wide[:, 128:], seen)
            halves.append(jnp.where(row % 2 == g, seen, pltpu.roll(seen, HEAD, 1)))
        parts[b, me] = jnp.where(lane < HEAD, *halves).astype(BF16)
        send(parts.at[b, me], part_send.at[b], part_recv.at[b])

    def finish(b):
        wait_peers(parts.at[b], part_recv.at[b])
        total = jnp.sum(parts[b].astype(F32), 0)
        out_ref[b, 0:HALF, :] = total[:, :HEAD].astype(BF16)
        out_ref[b, HALF:HEADS, :] = pltpu.roll(total, HEAD, 1)[:, :HEAD].astype(BF16)

    barrier = pltpu.get_barrier_semaphore()
    for b in range(SLOTS):
        k_copy(b, b).start()
    for peer in peers(me):
        pl.semaphore_signal(barrier, inc=1, device_id={"sp": peer}, device_id_type=MESH)

    empty = (jnp.zeros((HALF, 128), F32),) * 2

    def head(g, _):
        rows = empty
        for i in range(GROUP):
            b = GROUP * g + i
            rows = scores(b, b, i, rows)
            k_copy(b + SLOTS, b).start()
            v_copy(b, b).start()

        @pl.when(g == 0)
        def _():
            pl.semaphore_wait(barrier, DEV - 1)

        exchange(g, rows)
        return 0

    lax.fori_loop(0, AHEAD, head, 0)

    def body(g, _):
        share = shares(g)
        rows = empty
        for i in range(GROUP):
            b = GROUP * g + i
            slot = b % SLOTS
            rows = scores(b + LAG, slot, i, rows)
            values(b, slot, i, share)
        exchange(g + AHEAD, rows)
        for i in range(GROUP):
            b = GROUP * g + i
            slot = b % SLOTS
            v_copy(b + SLOTS, slot).start()

            @pl.when(b + LAG + SLOTS < SEQ)
            def _():
                k_copy(b + LAG + SLOTS, slot).start()

        @pl.when(g >= 2)
        def _():
            for i in range(GROUP):
                finish(GROUP * (g - 2) + i)

        return 0

    lax.fori_loop(0, GROUPS - AHEAD, body, 0)

    def tail(g, _):
        share = shares(g)
        for i in range(GROUP):
            b = GROUP * g + i
            values(b, b % SLOTS, i, share)
        return 0

    lax.fori_loop(GROUPS - AHEAD, GROUPS, tail, 0)

    def last(b, _):
        finish(b)
        return 0

    lax.fori_loop(GROUP * (GROUPS - AHEAD - 2), SEQ, last, 0)

    def drain(b, _):
        wait_peers(parts.at[b], part_send.at[b])
        return 0

    lax.fori_loop(0, SEQ, drain, 0)
    for g in range(GROUPS):
        wait_peers(stats.at[g], stat_send.at[g])


def solution(mesh):
    def step(q, k, v):
        k, v = (x.transpose(0, 2, 3, 1).reshape(SEQ, HEADS * HEAD, RUN) for x in (k, v))
        return pl.pallas_call(
            kernel,
            out_shape=jax.ShapeDtypeStruct(q.shape, BF16),
            in_specs=[pl.BlockSpec(memory_space=pltpu.VMEM)] + [pl.BlockSpec(memory_space=pl.ANY)] * 2,
            out_specs=pl.BlockSpec(memory_space=pltpu.VMEM),
            scratch_shapes=[
                pltpu.VMEM((SLOTS, HEADS * HEAD, RUN), BF16),
                pltpu.VMEM((SLOTS, HEADS * HEAD, RUN), BF16),
                pltpu.VMEM((SEQ, 2, HALF, RUN), F32),
                pltpu.VMEM((GROUPS, DEV, 1, 256), F32),
                pltpu.VMEM((SEQ, DEV, HALF, 128), BF16),
                pltpu.SemaphoreType.DMA((SLOTS,)),
                pltpu.SemaphoreType.DMA((SLOTS,)),
                pltpu.SemaphoreType.DMA((GROUPS,)),
                pltpu.SemaphoreType.DMA((GROUPS,)),
                pltpu.SemaphoreType.DMA((SEQ,)),
                pltpu.SemaphoreType.DMA((SEQ,)),
            ],
            compiler_params=pltpu.CompilerParams(collective_id=0, has_side_effects=True, vmem_limit_bytes=50 * 2**20),
            name="attend",
        )(q, k, v)

    return jax.shard_map(
        step,
        mesh=mesh,
        in_specs=(P("dp", None, None), P("dp", "sp", None, None), P("dp", "sp", None, None)),
        out_specs=P("dp", None, None),
        check_vma=False,
    )
```

time: 142 us -> 58.7 us (0.41)
  Pallas kernels: 0 us -> 56.9 us
  waiting for transfers between devices: 51.6 us -> 0 us
  matrix products: 48.3 us -> 0 us
  local copies, waits for them, and re-layouts: 15.5 us -> 1.65 us
  between operations: 13.4 us -> 0.01 us
  other arithmetic: 12.4 us -> 0 us
    pallas_call x0 -> x1, Pallas kernels: none -> 56.9 us  [step(): pl.pallas_call(kernel, out_shape=jax.ShapeDtypeStruct(q.shape, BF16), in_...]
    all_gather x1 -> x0, waiting for transfers between devices: 51.6 us -> none  [step(): return together(lax.all_gather(part_of(q, k, v), 'sp')).reshape(q.shape)]
    dot_general x2 -> x0, matrix products: 48.3 us -> none  [einsum(): return jnp.einsum(form, a.astype(jnp.float32), b.astype(jnp.float32))]
    all_gather x1 -> x0, local copies, waits for them, and re-layouts: 13.7 us -> none  [step(): return together(lax.all_gather(part_of(q, k, v), 'sp')).reshape(q.shape)]
    reduce_sum x2 -> x0, other arithmetic: 9.29 us -> none  [the longest x1 8.2 us: together(): jnp.sum(seen * scale, 0) / jnp.sum(total * scale, 0)]
    unnamed x0 -> x3, local copies, waits for them, and re-layouts: none -> 1.65 us
  transfers between devices with their start and end apart: 1 -> 0, of which waited for: 1 -> 0; matrix products, arithmetic and copies ran while one was open for 0% -> 0% of each run, Pallas kernels for 0% -> 0%
where the time goes in v1:
time: 58.7 us; the launch traced here: 58.6 us
  Pallas kernels  56.9 us (97%)
  local copies, waits for them, and re-layouts  1.65 us (3%)
    pallas_call x1, Pallas kernels, step(): pl.pallas_call(kernel, out_shape=jax.ShapeDtypeStruct(q.shape, BF16), in_...  56.9 us
    unnamed x3, local copies, waits for them, and re-layouts  1.65 us

profile of v1, /device:TPU:0, one launch (start us, length us, event | category | flops | bytes accessed | tf_op | source)
XLA Modules:
  0.0 58.6 jit_solution(18411849921414789240)
XLA Ops:
  0.0 0.0 copy-start
  0.0 0.9 %copy-done = bf16[32,32,64]{2,1,0:T(8,128)(2,1)S(1)} copy-done((bf16[32,32,64]{2,1,0:T(8,128)(2,1)S(1)}, bf16[32,32,64]{2,1,0:T(8,128)(2,1)}, u32[]{:S(2)}) %copy-start) | copy-done | bytes 131096
  1.0 56.9 %attend.1 = bf16[32,32,64]{2,1,0:T(8,128)(2,1)S(1)} custom-call(bf16[32,32,64]{2,1,0:T(8,128)(2,1)S(1)} %copy-done, bf16[32,2048,512]{2,1,0:T(8,128)(2,1)} %bitcast.1.k_ref, bf16[32,2048,512]{2,1,0:T(8,128)(2,1)} %bitcast.3.v_ref), custom_call_target="tpu_custom_call" | custom-call | tf_op jit(solution)/shard_map/attend/pallas_call | solution.py:181
  57.9 0.7 %copy.5 = bf16[32,32,64]{2,1,0:T(8,128)(2,1)} copy(bf16[32,32,64]{2,1,0:T(8,128)(2,1)S(1)} %attend.1) | data formatting | bytes 262144
Async XLA Ops:
  0.0 0.9 %copy-start = (bf16[32,32,64]{2,1,0:T(8,128)(2,1)S(1)}, bf16[32,32,64]{2,1,0:T(8,128)(2,1)}, u32[]{:S(2)}) copy-start(bf16[32,32,64]{2,1,0:T(8,128)(2,1)} %q_ref.1) | copy-start | bytes 393220

commit v2 on v0

v2 whole, which is shorter than its diff:
```python
import jax
import jax.numpy as jnp
from jax import lax
from jax.experimental import pallas as pl
from jax.experimental.pallas import tpu as pltpu
from jax.sharding import PartitionSpec as P

MESH = pl.DeviceIdType.MESH
BF16, F32 = jnp.bfloat16, jnp.float32

DEV = 16
SEQ = 32
PAIRS = SEQ // 2
HEADS = 32
HEAD = 64
RUN = 512
HALF = 16
ROWS = HALF * HEAD
LAG = 3
AHEAD = 2
SLOTS = 2 * (AHEAD + 1)
BUNCH = 4
BUNCHES = 3
DIRECT = PAIRS - BUNCH * BUNCHES
RAW = 3


def peers(me):
    bits = [(me // 2**i) % 2 for i in range(4)]
    for flip in (14, 15, 12, 10, 6, 13, 11, 7, 8, 4, 2, 9, 5, 3, 1):
        yield sum((1 - bit if flip >> i & 1 else bit) * 2**i for i, bit in enumerate(bits))


def kernel(q_ref, k_ref, v_ref, out_ref, qbuf, kbuf, vbuf, weights, raw, stats, cut, came, summed, parts, qsem, ksem, vsem, stat_send, stat_recv, cut_send, cut_recv, sum_send, sum_recv, part_send, part_recv):
    me = lax.axis_index("sp")
    row = lax.broadcasted_iota(jnp.int32, (HALF, 128), 0)
    lane = lax.broadcasted_iota(jnp.int32, (HALF, 128), 1)

    def k_copy(b):
        return pltpu.make_async_copy(k_ref.at[b], kbuf.at[b % SLOTS], ksem.at[b % SLOTS])

    def v_copy(b):
        return pltpu.make_async_copy(v_ref.at[b], vbuf.at[b % SLOTS], vsem.at[b % SLOTS])

    def start(copy, p):
        for i in range(2):
            copy(2 * p + i).start()

    def wait(copy, p):
        for i in range(2):
            copy(2 * p + i).wait()

    def send(ref, send_sem, recv_sem):
        for peer in peers(me):
            pltpu.make_async_remote_copy(ref, ref, send_sem, recv_sem, device_id={"sp": peer}, device_id_type=MESH).start()

    def wait_peers(ref, sem):
        some = ref.at[pl.ds(0, DEV - 1)]
        pltpu.make_async_copy(some, some, sem).wait()

    def scores(p):
        highs = sums = jnp.zeros((HALF, 128), F32)
        for i in range(2):
            b = 2 * p + i
            for g in range(2):
                query = qbuf[b, HALF * g : HALF * (g + 1), :].astype(F32)
                query = jnp.concatenate([query, query], -1)
                query = jnp.where(lane // HEAD == row % 2, query, 0.0)
                query = jnp.concatenate([jnp.where(row // 2 == c, query, 0.0).astype(BF16) for c in range(HALF // 2)], -1)
                score = jnp.dot(query, kbuf[b % SLOTS, ROWS * g : ROWS * (g + 1), :], preferred_element_type=F32) * HEAD**-0.5
                high = jnp.max(score, -1, keepdims=True)
                weight = jnp.exp(score - high)
                weights[b, g] = weight.astype(BF16)
                here = lane // HALF == 2 * i + g
                highs = jnp.where(here, high, highs)
                sums = jnp.where(here, jnp.sum(weight, -1, keepdims=True), sums)
        mine = lane % HALF == row
        stats[p, me, :, 0:128] = jnp.sum(jnp.where(mine, highs, 0.0), 0, keepdims=True)
        stats[p, me, :, 128:256] = jnp.sum(jnp.where(mine, sums, 0.0), 0, keepdims=True)

    def send_stats(p):
        send(stats.at[p, me], stat_send.at[p], stat_recv.at[p])

    def wait_stats(p):
        wait_peers(stats.at[p], stat_recv.at[p])

    def values(p, i):
        b = 2 * p + i
        for g in range(2):
            seen = jnp.zeros((HALF, 128), F32)
            for c in range(0, HALF // 2, 2):
                first = ROWS * g + 128 * c
                wide = lax.dot_general(weights[b, g], vbuf[b % SLOTS, first : first + 256, :], (((1,), (1,)), ((), ())), preferred_element_type=F32)
                seen = jnp.where(row // 2 == c, wide[:, :128], seen)
                seen = jnp.where(row // 2 == c + 1, wide[:, 128:], seen)
            raw[p % RAW, i, g] = seen

    def weigh(p, direct=False):
        high = stats[p, :, :, 0:128]
        top = jnp.max(high, 0)
        total = jnp.sum(stats[p, :, :, 128:256] * jnp.exp(high - top[None]), 0)
        share = jnp.exp(stats[p, me, :, 0:128] - top) / total
        for i in range(2):
            halves = []
            for g in range(2):
                scale = jnp.sum(jnp.where(lane == HALF * (2 * i + g) + row, share, 0.0), -1, keepdims=True)
                seen = raw[p % RAW, i, g] * scale
                halves.append(jnp.where(row % 2 == g, seen, pltpu.roll(seen, HEAD, 1)))
            seen = jnp.where(lane < HEAD, *halves).astype(BF16)
            if direct:
                parts[p - BUNCH * BUNCHES, me, i] = seen
            else:
                for g in range(2):
                    cut[p // BUNCH, 4 * (p % BUNCH) + 2 * i + g] = seen[8 * g : 8 * (g + 1)]

    def send_part(p):
        p = p - BUNCH * BUNCHES
        send(parts.at[p, me], part_send.at[p], part_recv.at[p])

    def send_cut(r):
        for peer in peers(me):
            pltpu.make_async_remote_copy(cut.at[r, peer], came.at[r, me], cut_send.at[r], cut_recv.at[r], device_id={"sp": peer}, device_id_type=MESH).start()

    def add_up(r):
        came[r, me] = cut[r, me]
        wait_peers(came.at[r], cut_recv.at[r])
        summed[r, me] = jnp.sum(came[r].astype(F32), 0).astype(BF16)
        send(summed.at[r, me], sum_send.at[r], sum_recv.at[r])

    def store(b, total):
        out_ref[b, 0:HALF, :] = total[:, :HEAD].astype(BF16)
        out_ref[b, HALF:HEADS, :] = pltpu.roll(total, HEAD, 1)[:, :HEAD].astype(BF16)

    def finish_bunch(r):
        wait_peers(summed.at[r], sum_recv.at[r])
        for i in range(2 * BUNCH):
            store(2 * BUNCH * r + i, jnp.concatenate([summed[r, 2 * i], summed[r, 2 * i + 1]], 0).astype(F32))

    def finish(p):
        p = p - BUNCH * BUNCHES
        wait_peers(parts.at[p], part_recv.at[p])
        for i in range(2):
            store(2 * (p + BUNCH * BUNCHES) + i, jnp.sum(parts[p, :, i].astype(F32), 0))

    q_copy = pltpu.make_async_copy(q_ref, qbuf, qsem)
    q_copy.start()
    for p in range(AHEAD):
        start(k_copy, p)
    barrier = pltpu.get_barrier_semaphore()
    for peer in peers(me):
        pl.semaphore_signal(barrier, inc=1, device_id={"sp": peer}, device_id_type=MESH)
    q_copy.wait()

    for p in range(LAG):
        wait(k_copy, p)
        start(k_copy, p + AHEAD)
        if p >= LAG - AHEAD:
            start(v_copy, p - LAG + AHEAD)
        scores(p)
    pl.semaphore_wait(barrier, DEV - 1)
    for p in range(LAG):
        send_stats(p)

    def both(p, more=True, due=(0,), direct=False):
        wait(k_copy, p + LAG)
        wait(v_copy, p)
        for d in due:
            wait_stats(p - d)
        if more:
            start(k_copy, p + LAG + AHEAD)
        start(v_copy, p + AHEAD)
        scores(p + LAG)
        for i in range(2):
            values(p, i)
        for d in due:
            weigh(p - d, direct)
        send_stats(p + LAG)

    both(0, due=())
    both(1, due=())
    both(2, due=(2, 1))
    both(3, due=(1, 0))
    send_cut(0)

    def middle(p, _):
        both(p)

        @pl.when(p % BUNCH == BUNCH - 1)
        def _():
            send_cut(p // BUNCH)

        @pl.when(p % BUNCH == 1)
        def _():
            add_up(p // BUNCH - 1)

        return 0

    turn = PAIRS - LAG - AHEAD
    lax.fori_loop(4, turn, middle, 0)
    for p in range(turn, turn + AHEAD):
        both(p, more=False, direct=p >= BUNCH * BUNCHES)
        if p >= BUNCH * BUNCHES:
            send_part(p)
        elif p % BUNCH == BUNCH - 1:
            send_cut(p // BUNCH)

    for p in range(PAIRS - LAG, PAIRS - 1):
        wait(v_copy, p)
        wait_stats(p)
        if p + AHEAD < PAIRS:
            start(v_copy, p + AHEAD)
        for i in range(2):
            values(p, i)
        weigh(p, True)
        send_part(p)
        if p == PAIRS - LAG:
            add_up(BUNCHES - 1)
    p = PAIRS - 1
    v_copy(2 * p).wait()
    values(p, 0)
    v_copy(2 * p + 1).wait()
    values(p, 1)
    wait_stats(p)
    weigh(p, True)
    send_part(p)

    for r in range(BUNCHES):
        finish_bunch(r)
        wait_peers(summed.at[r], sum_send.at[r])
        wait_peers(cut.at[r], cut_send.at[r])

    def drain(p, _):
        wait_peers(stats.at[p], stat_send.at[p])
        return 0

    lax.fori_loop(0, PAIRS, drain, 0)
    for p in range(PAIRS - DIRECT, PAIRS):
        finish(p)
    for p in range(DIRECT):
        wait_peers(parts.at[p], part_send.at[p])


def solution(mesh):
    def step(q, k, v):
        k, v = (x.transpose(0, 2, 3, 1).reshape(SEQ, HEADS * HEAD, RUN) for x in (k, v))
        return pl.pallas_call(
            kernel,
            out_shape=jax.ShapeDtypeStruct(q.shape, BF16),
            in_specs=[pl.BlockSpec(memory_space=pltpu.HBM)] * 3,
            out_specs=pl.BlockSpec(memory_space=pltpu.VMEM),
            scratch_shapes=[
                pltpu.VMEM(q.shape, BF16),
                pltpu.VMEM((SLOTS, HEADS * HEAD, RUN), BF16),
                pltpu.VMEM((SLOTS, HEADS * HEAD, RUN), BF16),
                pltpu.VMEM((SEQ, 2, HALF, RUN), BF16),
                pltpu.VMEM((RAW, 2, 2, HALF, 128), F32),
                pltpu.VMEM((PAIRS, DEV, 1, 256), F32),
                pltpu.VMEM((BUNCHES, DEV, 8, 128), BF16),
                pltpu.VMEM((BUNCHES, DEV, 8, 128), BF16),
                pltpu.VMEM((BUNCHES, DEV, 8, 128), BF16),
                pltpu.VMEM((DIRECT, DEV, 2, HALF, 128), BF16),
                pltpu.SemaphoreType.DMA,
                pltpu.SemaphoreType.DMA((SLOTS,)),
                pltpu.SemaphoreType.DMA((SLOTS,)),
                pltpu.SemaphoreType.DMA((PAIRS,)),
                pltpu.SemaphoreType.DMA((PAIRS,)),
                pltpu.SemaphoreType.DMA((BUNCHES,)),
                pltpu.SemaphoreType.DMA((BUNCHES,)),
                pltpu.SemaphoreType.DMA((BUNCHES,)),
                pltpu.SemaphoreType.DMA((BUNCHES,)),
                pltpu.SemaphoreType.DMA((DIRECT,)),
                pltpu.SemaphoreType.DMA((DIRECT,)),
            ],
            compiler_params=pltpu.CompilerParams(collective_id=0, has_side_effects=True, vmem_limit_bytes=50 * 2**20),
            name="attend",
        )(q, k, v)

    return jax.shard_map(
        step,
        mesh=mesh,
        in_specs=(P("dp", None, None), P("dp", "sp", None, None), P("dp", "sp", None, None)),
        out_specs=P("dp", None, None),
        check_vma=False,
    )
```

time: 142 us -> 51.8 us (0.36)
  waiting for transfers between devices: 51.6 us -> 0 us
  Pallas kernels: 0 us -> 50 us
  matrix products: 48.3 us -> 0 us
  local copies, waits for them, and re-layouts: 15.5 us -> 1.65 us
  between operations: 13.4 us -> 0.01 us
  other arithmetic: 12.4 us -> 0 us
    all_gather x1 -> x0, waiting for transfers between devices: 51.6 us -> none  [step(): return together(lax.all_gather(part_of(q, k, v), 'sp')).reshape(q.shape)]
    pallas_call x0 -> x1, Pallas kernels: none -> 50 us  [step(): pl.pallas_call(kernel, out_shape=jax.ShapeDtypeStruct(q.shape, BF16), in_...]
    dot_general x2 -> x0, matrix products: 48.3 us -> none  [einsum(): return jnp.einsum(form, a.astype(jnp.float32), b.astype(jnp.float32))]
    all_gather x1 -> x0, local copies, waits for them, and re-layouts: 13.7 us -> none  [step(): return together(lax.all_gather(part_of(q, k, v), 'sp')).reshape(q.shape)]
    reduce_sum x2 -> x0, other arithmetic: 9.29 us -> none  [the longest x1 8.2 us: together(): jnp.sum(seen * scale, 0) / jnp.sum(total * scale, 0)]
    unnamed x0 -> x3, local copies, waits for them, and re-layouts: none -> 1.65 us
  transfers between devices with their start and end apart: 1 -> 0, of which waited for: 1 -> 0; matrix products, arithmetic and copies ran while one was open for 0% -> 0% of each run, Pallas kernels for 0% -> 0%
where the time goes in v2:
time: 51.8 us; the launch traced here: 51.6 us
  Pallas kernels  50 us (97%)
  local copies, waits for them, and re-layouts  1.65 us (3%)
    pallas_call x1, Pallas kernels, step(): pl.pallas_call(kernel, out_shape=jax.ShapeDtypeStruct(q.shape, BF16), in_...  50 us
    unnamed x3, local copies, waits for them, and re-layouts  1.65 us

profile of v2, /device:TPU:0, one launch (start us, length us, event | category | flops | bytes accessed | tf_op | source)
XLA Modules:
  0.0 51.6 jit_solution(7710233885267132228)
XLA Ops:
  0.0 0.0 copy-start
  0.0 0.9 %copy-done = bf16[32,32,64]{2,1,0:T(8,128)(2,1)S(1)} copy-done((bf16[32,32,64]{2,1,0:T(8,128)(2,1)S(1)}, bf16[32,32,64]{2,1,0:T(8,128)(2,1)}, u32[]{:S(2)}) %copy-start) | copy-done | bytes 131096
  1.0 50.0 %attend.1 = bf16[32,32,64]{2,1,0:T(8,128)(2,1)S(1)} custom-call(bf16[32,32,64]{2,1,0:T(8,128)(2,1)S(1)} %copy-done, bf16[32,2048,512]{2,1,0:T(8,128)(2,1)} %bitcast.1.k_ref, bf16[32,2048,512]{2,1,0:T(8,128)(2,1)} %bitcast.3.v_ref), custom_call_target="tpu_custom_call" | custom-call | tf_op jit(solution)/shard_map/attend/pallas_call | solution.py:246
  50.9 0.7 %copy.5 = bf16[32,32,64]{2,1,0:T(8,128)(2,1)} copy(bf16[32,32,64]{2,1,0:T(8,128)(2,1)S(1)} %attend.1) | data formatting | bytes 262144
Async XLA Ops:
  0.0 0.9 %copy-start = (bf16[32,32,64]{2,1,0:T(8,128)(2,1)S(1)}, bf16[32,32,64]{2,1,0:T(8,128)(2,1)}, u32[]{:S(2)}) copy-start(bf16[32,32,64]{2,1,0:T(8,128)(2,1)} %q_ref.1) | copy-start | bytes 393220

commit v3 on v2

--- a/solution.py
+++ b/solution.py
@@ -58,22 +58,27 @@
         some = ref.at[pl.ds(0, DEV - 1)]
         pltpu.make_async_copy(some, some, sem).wait()
 
-    def scores(p):
-        highs = sums = jnp.zeros((HALF, 128), F32)
-        for i in range(2):
-            b = 2 * p + i
-            for g in range(2):
-                query = qbuf[b, HALF * g : HALF * (g + 1), :].astype(F32)
-                query = jnp.concatenate([query, query], -1)
-                query = jnp.where(lane // HEAD == row % 2, query, 0.0)
-                query = jnp.concatenate([jnp.where(row // 2 == c, query, 0.0).astype(BF16) for c in range(HALF // 2)], -1)
-                score = jnp.dot(query, kbuf[b % SLOTS, ROWS * g : ROWS * (g + 1), :], preferred_element_type=F32) * HEAD**-0.5
-                high = jnp.max(score, -1, keepdims=True)
-                weight = jnp.exp(score - high)
-                weights[b, g] = weight.astype(BF16)
-                here = lane // HALF == 2 * i + g
-                highs = jnp.where(here, high, highs)
-                sums = jnp.where(here, jnp.sum(weight, -1, keepdims=True), sums)
+    nothing = (jnp.zeros((HALF, 128), F32),) * 2
+
+    def scores(p, i, found):
+        highs, sums = found
+        b = 2 * p + i
+        for g in range(2):
+            query = qbuf[b, HALF * g : HALF * (g + 1), :].astype(F32)
+            query = jnp.concatenate([query, query], -1)
+            query = jnp.where(lane // HEAD == row % 2, query, 0.0)
+            query = jnp.concatenate([jnp.where(row // 2 == c, query, 0.0).astype(BF16) for c in range(HALF // 2)], -1)
+            score = jnp.dot(query, kbuf[b % SLOTS, ROWS * g : ROWS * (g + 1), :], preferred_element_type=F32) * HEAD**-0.5
+            high = jnp.max(score, -1, keepdims=True)
+            weight = jnp.exp(score - high)
+            weights[b, g] = weight.astype(BF16)
+            here = lane // HALF == 2 * i + g
+            highs = jnp.where(here, high, highs)
+            sums = jnp.where(here, jnp.sum(weight, -1, keepdims=True), sums)
+        return highs, sums
+
+    def note(p, found):
+        highs, sums = found
         mine = lane % HALF == row
         stats[p, me, :, 0:128] = jnp.sum(jnp.where(mine, highs, 0.0), 0, keepdims=True)
         stats[p, me, :, 128:256] = jnp.sum(jnp.where(mine, sums, 0.0), 0, keepdims=True)
@@ -156,40 +161,49 @@
         start(k_copy, p + AHEAD)
         if p >= LAG - AHEAD:
             start(v_copy, p - LAG + AHEAD)
-        scores(p)
+        found = nothing
+        for i in range(2):
+            found = scores(p, i, found)
+        note(p, found)
     pl.semaphore_wait(barrier, DEV - 1)
     for p in range(LAG):
         send_stats(p)
 
-    def both(p, more=True, due=(0,), direct=False):
-        wait(k_copy, p + LAG)
-        wait(v_copy, p)
-        for d in due:
+    def both(p, more=True, due=(1,), late=()):
+        for d in due + late:
             wait_stats(p - d)
-        if more:
-            start(k_copy, p + LAG + AHEAD)
-        start(v_copy, p + AHEAD)
-        scores(p + LAG)
-        for i in range(2):
+        found = nothing
+        for i in range(2):
+            k_copy(2 * (p + LAG) + i).wait()
+            v_copy(2 * p + i).wait()
+            if i == 0:
+                for j in range(2):
+                    if more:
+                        k_copy(2 * (p + LAG + AHEAD) + j).start()
+                    v_copy(2 * (p + AHEAD) + j).start()
+            found = scores(p + LAG, i, found)
             values(p, i)
-        for d in due:
-            weigh(p - d, direct)
+            if i == 0:
+                for d in due:
+                    weigh(p - d)
+        note(p + LAG, found)
+        for d in late:
+            weigh(p - d)
         send_stats(p + LAG)
 
     both(0, due=())
     both(1, due=())
     both(2, due=(2, 1))
-    both(3, due=(1, 0))
-    send_cut(0)
+    both(3)
 
     def middle(p, _):
         both(p)
 
-        @pl.when(p % BUNCH == BUNCH - 1)
+        @pl.when(p % BUNCH == 0)
         def _():
-            send_cut(p // BUNCH)
-
-        @pl.when(p % BUNCH == 1)
+            send_cut(p // BUNCH - 1)
+
+        @pl.when(p % BUNCH == 2)
         def _():
             add_up(p // BUNCH - 1)
 
@@ -197,32 +211,25 @@
 
     turn = PAIRS - LAG - AHEAD
     lax.fori_loop(4, turn, middle, 0)
-    for p in range(turn, turn + AHEAD):
-        both(p, more=False, direct=p >= BUNCH * BUNCHES)
-        if p >= BUNCH * BUNCHES:
-            send_part(p)
-        elif p % BUNCH == BUNCH - 1:
-            send_cut(p // BUNCH)
-
-    for p in range(PAIRS - LAG, PAIRS - 1):
+    both(turn, more=False, late=(0,))
+    send_cut(BUNCHES - 1)
+    both(turn + 1, more=False, due=())
+
+    for p in range(PAIRS - LAG, PAIRS):
         wait(v_copy, p)
-        wait_stats(p)
+        wait_stats(p - 1)
+        if p == PAIRS - 1:
+            wait_stats(p)
         if p + AHEAD < PAIRS:
             start(v_copy, p + AHEAD)
-        for i in range(2):
-            values(p, i)
-        weigh(p, True)
-        send_part(p)
-        if p == PAIRS - LAG:
+        values(p, 0)
+        weigh(p - 1, True)
+        send_part(p - 1)
+        values(p, 1)
+        if p == PAIRS - 3:
             add_up(BUNCHES - 1)
-    p = PAIRS - 1
-    v_copy(2 * p).wait()
-    values(p, 0)
-    v_copy(2 * p + 1).wait()
-    values(p, 1)
-    wait_stats(p)
-    weigh(p, True)
-    send_part(p)
+    weigh(PAIRS - 1, True)
+    send_part(PAIRS - 1)
 
     for r in range(BUNCHES):
         finish_bunch(r)
@@ -234,15 +241,15 @@
         return 0
 
     lax.fori_loop(0, PAIRS, drain, 0)
-    for p in range(PAIRS - DIRECT, PAIRS):
-        finish(p)
     for p in range(DIRECT):
         wait_peers(parts.at[p], part_send.at[p])
+        finish(p + PAIRS - DIRECT)
 
 
 def solution(mesh):
     def step(q, k, v):
         k, v = (x.transpose(0, 2, 3, 1).reshape(SEQ, HEADS * HEAD, RUN) for x in (k, v))
+        q = pltpu.with_memory_space_constraint(q, pltpu.HBM)
         return pl.pallas_call(
             kernel,
             out_shape=jax.ShapeDtypeStruct(q.shape, BF16),

time: 51.8 us -> 51.1 us (0.986)
  local copies, waits for them, and re-layouts: 1.65 us -> 0.71 us
    unnamed x3 -> x1, local copies, waits for them, and re-layouts: 1.65 us -> 0.71 us
where the time goes in v3:
time: 51.1 us; the launch traced here: 51 us
  Pallas kernels  50.3 us (98%)
  local copies, waits for them, and re-layouts  0.71 us (1%)
    pallas_call x1, Pallas kernels, step(): pl.pallas_call(kernel, out_shape=jax.ShapeDtypeStruct(q.shape, BF16), in_...  50.3 us

profile of v3, /device:TPU:0, one launch (start us, length us, event | category | flops | bytes accessed | tf_op | source)
XLA Modules:
  0.0 51.0 jit_solution(7566876068200687950)
XLA Ops:
  0.0 50.3 %attend.1 = bf16[32,32,64]{2,1,0:T(8,128)(2,1)S(1)} custom-call(bf16[32,32,64]{2,1,0:T(8,128)(2,1)} %q_ref.1, bf16[32,2048,512]{2,1,0:T(8,128)(2,1)} %bitcast.1.k_ref, bf16[32,2048,512]{2,1,0:T(8,128)(2,1)} %bitcast.3.v_ref), custom_call_target="tpu_custom_call" | custom-call | tf_op jit(solution)/shard_map/attend/pallas_call | solution.py:253
  50.3 0.7 %copy.5 = bf16[32,32,64]{2,1,0:T(8,128)(2,1)} copy(bf16[32,32,64]{2,1,0:T(8,128)(2,1)S(1)} %attend.1) | data formatting | bytes 262144

commit v4 on v3

--- a/solution.py
+++ b/solution.py
@@ -218,13 +218,13 @@
     for p in range(PAIRS - LAG, PAIRS):
         wait(v_copy, p)
         wait_stats(p - 1)
-        if p == PAIRS - 1:
-            wait_stats(p)
         if p + AHEAD < PAIRS:
             start(v_copy, p + AHEAD)
         values(p, 0)
         weigh(p - 1, True)
         send_part(p - 1)
+        if p == PAIRS - 1:
+            wait_stats(p)
         values(p, 1)
         if p == PAIRS - 3:
             add_up(BUNCHES - 1)

time: 51.1 us -> 51.1 us (level)
  no operation moved by 1% of the time
where the time goes in v4:
time: 51.1 us; the launch traced here: 51 us
  Pallas kernels  50.3 us (98%)
  local copies, waits for them, and re-layouts  0.71 us (1%)
    pallas_call x1, Pallas kernels, step(): pl.pallas_call(kernel, out_shape=jax.ShapeDtypeStruct(q.shape, BF16), in_...  50.3 us

profile of v4, /device:TPU:0, one launch (start us, length us, event | category | flops | bytes accessed | tf_op | source)
XLA Modules:
  0.0 51.0 jit_solution(973917572208125824)
XLA Ops:
  0.0 50.3 %attend.1 = bf16[32,32,64]{2,1,0:T(8,128)(2,1)S(1)} custom-call(bf16[32,32,64]{2,1,0:T(8,128)(2,1)} %q_ref.1, bf16[32,2048,512]{2,1,0:T(8,128)(2,1)} %bitcast.1.k_ref, bf16[32,2048,512]{2,1,0:T(8,128)(2,1)} %bitcast.3.v_ref), custom_call_target="tpu_custom_call" | custom-call | tf_op jit(solution)/shard_map/attend/pallas_call | solution.py:253
  50.3 0.7 %copy.5 = bf16[32,32,64]{2,1,0:T(8,128)(2,1)} copy(bf16[32,32,64]{2,1,0:T(8,128)(2,1)S(1)} %attend.1) | data formatting | bytes 262144
